TPU v7x, 256 devices: a whole 4x4x8 slice. The times are simulated.
256 devices in a mesh: section: 8 (over y, x_hi), ep: 32 (over z, x_lo, core).
Axes of the slice: x: 4 (x_hi: 2, x_lo: 2; x = x_hi * 2 + x_lo), y: 4, z: 8, core: 2. Of those that a mesh axis runs over, the one named last changes fastest.
Arguments:
- handed: bfloat16 [8, 2, 2048, 7168], P('section', None, 'ep'), may hold values from -6 to 6
- routes: int32 [8, 2, 2048, 2], P('section', None, 'ep'), may hold values from 0 to 3, all different within a row; in each aligned block of 64 rows (0 to 63, 64 to 127, ..., all dimensions but the last counted through in order) at most 36 rows name the same one
- slot_order: int32 [8, 2, 32, 64], P('section', None, 'ep'), may hold values from 0 to 63, each once within a row
- gate_probs: float32 [8, 2, 2048, 2], P('section', None, 'ep'), may hold values from 0.2 to 1
- saved_gate: bfloat16 [8, 2, 32, 32, 36, 128], P('section', None, 'ep'), may hold values from -6 to 6
- saved_up: bfloat16 [8, 2, 32, 32, 36, 128], P('section', None, 'ep'), may hold values from -6 to 6
- w_gate: bfloat16 [8, 32, 896, 1024], P('section', 'ep'), may hold values from -0.0625 to 0.0625
- w_up: bfloat16 [8, 32, 896, 1024], P('section', 'ep'), may hold values from -0.0625 to 0.0625
- w_down: bfloat16 [8, 32, 1024, 896], P('section', 'ep'), may hold values from -0.1875 to 0.1875
Outputs:
- grad_in: bfloat16 [8, 2, 2048, 7168], P('section', None, 'ep')
Inputs may be any that keep to these rules, and one draw needn't show every extreme that they name: `routes`: each row names 2 different experts; within the 64 rows of one device for one direction no expert is named by more than 36 rows, and in some such blocks one expert is named by exactly 36. `slot_order`: within one device and direction each of 0 to 63 stands once.
All inputs are finite; a program needn't handle non-finite values.
Results may differ from a plain program's by a relative error of at most 0.011.
Values may be sent and summed in bfloat16 or wider, within the bound.
A program may use at most 128 MiB of HBM per device.

v0:
```python
import jax
import jax.numpy as jnp
from jax import lax
from jax.sharding import PartitionSpec as P

EXPERTS = 4
TOPF = 2
CAP = 36


def passed_along(value, axis, steps):
    count = lax.axis_size(axis)
    pairs = [(source, (source + steps) % count) for source in range(count)]
    return lax.ppermute(value, axis, pairs)


def partner_2(value, axis, apart):
    mask = 2**apart
    pairs = [(source, source ^ mask) for source in range(lax.axis_size(axis))]
    return lax.ppermute(value, axis, pairs)


def slot_table(routing, sequence):
    expert_ids = jnp.arange(EXPERTS, dtype=jnp.int32)
    picked = (routing[:, :, None] == expert_ids[None, None, :]).astype(jnp.int32)
    named_count = jnp.sum(picked, axis=1)
    before = (sequence[None, :] < sequence[:, None]).astype(jnp.int32)
    counts = jnp.sum(before[:, :, None] * named_count[None, :, :], axis=1)
    return jnp.sum(counts[:, None, :] * picked, axis=2)


def take_rows(source, indices):
    return jnp.take(source, indices, axis=0)


def halve_sums(partial_value, group_size, bit_order, mover):
    batches, row_count, full_width = partial_value.shape
    levels = group_size.bit_length() - 1
    slice_width = full_width // group_size
    current = partial_value.reshape((batches, row_count) + (2,) * levels + (slice_width,))
    position = lax.axis_index("ep")
    for bit_index in bit_order:
        split_axis = 2 + levels - 1 - bit_index
        half_bit = position >> bit_index & 1
        kept_half = lax.dynamic_slice_in_dim(current, half_bit, 1, axis=split_axis)
        given_half = lax.dynamic_slice_in_dim(current, 1 - half_bit, 1, axis=split_axis)
        current = kept_half + mover(given_half, bit_index)
    return current.reshape(batches, row_count, slice_width)


def gather_parts(pieces, group_size, bit_order, mover):
    levels = group_size.bit_length() - 1
    leading_shape = pieces.shape[:-1]
    slice_width = pieces.shape[-1]
    current = pieces.reshape(leading_shape + (1,) * levels + (slice_width,))
    position = lax.axis_index("ep")
    base_axis = len(leading_shape)
    for bit_index in reversed(bit_order):
        split_axis = base_axis + levels - 1 - bit_index
        partner = mover(current, bit_index)
        half_bit = position >> bit_index & 1
        triple = jnp.concatenate([partner, current, partner], axis=split_axis)
        current = lax.dynamic_slice_in_dim(triple, 1 - half_bit, 2, axis=split_axis)
    return current.reshape(leading_shape + (slice_width * group_size,))


def expert_pass(
    grads, routing, sequence, probs_here, gate_act, up_act, weights, movers, group_size, bit_order
):
    w_gate, w_up, w_down = weights
    send_rows, swap_sums, swap_parts, send_back = movers
    batches, tokens, model_width = grads.shape
    slice_width = model_width // group_size
    gate_vals = gate_act.reshape(batches, -1, gate_act.shape[-1])
    up_vals = up_act.reshape(batches, -1, up_act.shape[-1])
    slots = jax.vmap(slot_table)(routing, sequence)
    target = (routing * CAP + slots).reshape(batches, tokens * TOPF)
    slot_ids = jnp.arange(EXPERTS * CAP, dtype=jnp.int32)
    hits = target[:, :, None] == slot_ids[None, None, :]
    token_ids = jnp.arange(tokens * TOPF, dtype=jnp.int32) // TOPF
    source_token = jnp.sum(jnp.where(hits, token_ids[None, :, None], 0), axis=1)
    slot_probs = jnp.sum(
        jnp.where(hits, probs_here.reshape(batches, tokens * TOPF)[:, :, None], 0.0), axis=1
    )
    block_ids = jnp.arange(group_size, dtype=jnp.int32)
    row_index = (
        source_token.reshape(batches, EXPERTS, 1, CAP) * group_size + block_ids[None, None, :, None]
    )
    flat_grads = grads.reshape(batches, tokens * group_size, slice_width)
    rows = jax.vmap(take_rows)(flat_grads, row_index.reshape(batches, -1))
    scale_rows = jnp.broadcast_to(
        slot_probs.reshape(batches, EXPERTS, 1, CAP), (batches, EXPERTS, group_size, CAP)
    )
    outgoing = (scale_rows.reshape(batches, -1)[:, :, None] * rows.astype(jnp.float32)).astype(
        jnp.bfloat16
    )
    outgoing = outgoing.reshape(batches, EXPERTS * group_size, CAP, slice_width)
    arrived = send_rows(outgoing)
    row_block = arrived.reshape(batches, -1, slice_width)
    partial_value = jnp.einsum("brd,fd->brf", row_block, w_down, preferred_element_type=jnp.float32)
    hidden_grad = halve_sums(partial_value, group_size, bit_order, swap_sums)
    gate_float = gate_vals.astype(jnp.float32)
    up_float = up_vals.astype(jnp.float32)
    sigma = jax.nn.sigmoid(gate_float)
    up_grad = (hidden_grad * gate_float * sigma).astype(jnp.bfloat16)
    gate_grad = (hidden_grad * up_float * sigma * (1.0 + gate_float * (1.0 - sigma))).astype(
        jnp.bfloat16
    )
    both_grads = gather_parts(jnp.stack([gate_grad, up_grad]), group_size, bit_order, swap_parts)
    result = jnp.einsum("brf,df->brd", both_grads[0], w_gate, preferred_element_type=jnp.float32)
    result = result + jnp.einsum(
        "brf,df->brd", both_grads[1], w_up, preferred_element_type=jnp.float32
    )
    result = result.astype(jnp.bfloat16).reshape(batches, EXPERTS * group_size, CAP, slice_width)
    returned = send_back(result).reshape(batches, EXPERTS * group_size * CAP, slice_width)
    back_index = (
        routing[:, :, :, None] * group_size + block_ids[None, None, None, :]
    ) * CAP + slots[:, :, :, None]
    picked = jax.vmap(take_rows)(returned, back_index.reshape(batches, -1))
    picked = picked.reshape(batches, tokens, TOPF, group_size, slice_width)
    summed = jnp.sum(picked.astype(jnp.float32), axis=2)
    return summed.astype(jnp.bfloat16).reshape(batches, tokens, model_width)


def local(handed, routes, slot_order, gate_probs, saved_gate, saved_up, w_gate, w_up, w_down):
    group_size = lax.axis_size("ep") // EXPERTS
    levels = group_size.bit_length() - 1
    bit_order = list(range(levels - 1, -1, -1))
    from_later = passed_along(handed[0, 0], "section", -1)
    from_earlier = passed_along(handed[0, 1], "section", 1)
    weights = (w_gate[0, 0], w_up[0, 0], w_down[0, 0])
    routing = routes[0]
    sequence = slot_order[0, :, 0]
    probs_here = gate_probs[0]
    gate_act = saved_gate[0, :, 0]
    up_act = saved_up[0, :, 0]
    movers = (
        lambda payload: lax.all_to_all(payload, "ep", split_axis=1, concat_axis=1, tiled=True),
        lambda payload, bit_index: partner_2(payload.astype(jnp.bfloat16), "ep", bit_index).astype(
            payload.dtype
        ),
        lambda payload, bit_index: partner_2(payload, "ep", bit_index),
        lambda payload: lax.all_to_all(payload, "ep", split_axis=1, concat_axis=1, tiled=True),
    )
    leading = expert_pass(
        from_later[None],
        routing[0:1],
        sequence[0:1],
        probs_here[0:1],
        gate_act[0:1],
        up_act[0:1],
        weights,
        movers,
        group_size,
        bit_order,
    )
    second = expert_pass(
        from_earlier[None],
        routing[1:2],
        sequence[1:2],
        probs_here[1:2],
        gate_act[1:2],
        up_act[1:2],
        weights,
        movers,
        group_size,
        bit_order,
    )
    result = jnp.concatenate([leading, second], axis=0)
    return result[None]


def solution(mesh):
    in_specs = (
        P("section", None, "ep", None),
        P("section", None, "ep", None),
        P("section", None, "ep", None),
        P("section", None, "ep", None),
        P("section", None, "ep", None, None, None),
        P("section", None, "ep", None, None, None),
        P("section", "ep", None, None),
        P("section", "ep", None, None),
        P("section", "ep", None, None),
    )
    out_specs = P("section", None, "ep", None)
    return jax.shard_map(local, mesh=mesh, in_specs=in_specs, out_specs=out_specs, check_vma=False)
```

profile of v0, /device:TPU:3, one launch (start us, length us, event | category | flops | bytes accessed | tf_op | source)
XLA Modules:
  0.0 541.0 jit_solution(3978668082111828133)
XLA Ops:
  2.6 4.3 collective-permute-start
  9.5 16.5 %collective-permute-done = bf16[64,7168]{1,0:T(8,128)(2,1)} collective-permute-done((bf16[64,7168]{1,0:T(8,128)(2,1)S(1)}, bf16[64,7168]{1,0:T(8,128)(2,1)}, u32[]{:S(2)}, u32[]{:S(2)}) %collective-permute-start) | collective-permute-done | bytes 917536 | tf_op jit(solution)/shard_map/ppermute | solution.py:14
  27.5 13.5 %gather_fusion = bf16[1152,896]{1,0:T(8,128)(2,1)} fusion(bf16[1,512,896]{2,1,0:T(8,128)(2,1)S(1)} %reshape_broadcast_in_dim.6, s32[1152]{0:T(1024)S(1)} %fusion.42), kind=kCustom, calls=%fused_computation.clone | custom fusion | bytes 4137984 | tf_op jit(solution)/shard_map/vmap(jit(_take))/gather | solution.py:33
  48.0 11.4 %all-to-all-start = ((bf16[1,32,36,896]{3,2,0,1:T(8,128)(2,1)}), bf16[1,32,36,896]{3,2,0,1:T(8,128)(2,1)}, u32[]{:S(2)}, u32[]{:S(2)}) async-start(bf16[1,32,36,896]{3,2,0,1:T(8,128)(2,1)} %bitcast.144), calls=%async_computation | async-start | bytes 4587520 | tf_op jit(solution)/shard_map/all_to_all | solution.py:138
  62.7 43.4 %collective-permute-done.7 = bf16[64,7168]{1,0:T(8,128)(2,1)} collective-permute-done((bf16[64,7168]{1,0:T(8,128)(2,1)S(1)}, bf16[64,7168]{1,0:T(8,128)(2,1)}, u32[]{:S(2)}, u32[]{:S(2)}) %collective-permute-start.7) | collective-permute-done | bytes 917536 | tf_op jit(solution)/shard_map/ppermute | solution.py:14
  107.6 13.6 %gather_fusion.2 = bf16[1152,896]{1,0:T(8,128)(2,1)} fusion(bf16[1,512,896]{2,1,0:T(8,128)(2,1)S(1)} %reshape_broadcast_in_dim.7, s32[1152]{0:T(1024)S(1)} %fusion.43), kind=kCustom, calls=%fused_computation.2.clone | custom fusion | bytes 4137984 | tf_op jit(solution)/shard_map/vmap(jit(_take))/gather | solution.py:33
  124.3 3.9 reshape.1131
  128.3 13.1 %all-to-all-start.2 = ((bf16[1,32,36,896]{3,2,0,1:T(8,128)(2,1)}), bf16[1,32,36,896]{3,2,0,1:T(8,128)(2,1)}, u32[]{:S(2)}, u32[]{:S(2)}) async-start(bf16[1,32,36,896]{3,2,0,1:T(8,128)(2,1)} %bitcast.143), calls=%async_computation.2 | async-start | bytes 4587520 | tf_op jit(solution)/shard_map/all_to_all | solution.py:138
  141.4 4.0 reshape.1197
  145.3 4.4 fusion.12
  153.4 43.4 %all-to-all-done.2 = bf16[1,32,36,896]{3,2,0,1:T(8,128)(2,1)} async-done(((bf16[1,32,36,896]{3,2,0,1:T(8,128)(2,1)}), bf16[1,32,36,896]{3,2,0,1:T(8,128)(2,1)}, u32[]{:S(2)}, u32[]{:S(2)}) %all-to-all-start.2) | async-done | bytes 2064416 | tf_op jit(solution)/shard_map/all_to_all | solution.py:138
  196.9 4.0 reshape.1198
  200.8 4.6 fusion.10
  205.4 12.2 %collective-permute-done.1 = bf16[1,1152,1,2,2,128]{1,5,4,3,2,0:T(8,128)(2,1)} collective-permute-done((bf16[1,1152,1,2,2,128]{1,5,4,3,2,0:T(8,128)(2,1)S(1)}, bf16[1,1152,1,2,2,128]{1,5,4,3,2,0:T(8,128)(2,1)}, u32[]{:S(2)}, u32[]{:S(2)}) %collective-permute-start.1) | collective-permute-done | bytes 1179680 | tf_op jit(solution)/shard_map/ppermute | solution.py:20
  227.9 6.5 %collective-permute-done.2 = bf16[1,1152,1,1,2,128]{1,5,4,3,2,0:T(8,128)(2,1)} collective-permute-done((bf16[1,1152,1,1,2,128]{1,5,4,3,2,0:T(8,128)(2,1)}, bf16[1,1152,1,1,2,128]{1,5,4,3,2,0:T(8,128)(2,1)}, u32[]{:S(2)}, u32[]{:S(2)}) %collective-permute-start.2) | collective-permute-done | bytes 589856 | tf_op jit(solution)/shard_map/ppermute | solution.py:20
  237.5 10.6 %collective-permute-done.8 = bf16[1,1152,1,2,2,128]{1,5,4,3,2,0:T(8,128)(2,1)} collective-permute-done((bf16[1,1152,1,2,2,128]{1,5,4,3,2,0:T(8,128)(2,1)}, bf16[1,1152,1,2,2,128]{1,5,4,3,2,0:T(8,128)(2,1)}, u32[]{:S(2)}, u32[]{:S(2)}) %collective-permute-start.8) | collective-permute-done | bytes 1179680 | tf_op jit(solution)/shard_map/ppermute | solution.py:20
  255.4 9.0 %collective-permute-done.9 = bf16[1,1152,1,1,2,128]{1,5,4,3,2,0:T(8,128)(2,1)} collective-permute-done((bf16[1,1152,1,1,2,128]{1,5,4,3,2,0:T(8,128)(2,1)}, bf16[1,1152,1,1,2,128]{1,5,4,3,2,0:T(8,128)(2,1)}, u32[]{:S(2)}, u32[]{:S(2)}) %collective-permute-start.9) | collective-permute-done | bytes 589856 | tf_op jit(solution)/shard_map/ppermute | solution.py:20
  278.2 15.0 %collective-permute-done.5 = bf16[2,1,1152,1,1,2,128]{2,6,0,5,4,3,1:T(8,128)(2,1)} collective-permute-done((bf16[2,1,1152,1,1,2,128]{2,6,0,5,4,3,1:T(8,128)(2,1)S(1)}, bf16[2,1,1152,1,1,2,128]{2,6,0,5,4,3,1:T(8,128)(2,1)}, u32[]{:S(2)}, u32[]{:S(2)}) %collective-permute-start.5) | collective-permute-done | bytes 1179680 | tf_op jit(solution)/shard_map/ppermute | solution.py:20
  298.3 24.0 %collective-permute-done.12 = bf16[2,1,1152,1,1,2,128]{2,6,0,5,4,3,1:T(8,128)(2,1)} collective-permute-done((bf16[2,1,1152,1,1,2,128]{2,6,0,5,4,3,1:T(8,128)(2,1)S(1)}, bf16[2,1,1152,1,1,2,128]{2,6,0,5,4,3,1:T(8,128)(2,1)}, u32[]{:S(2)}, u32[]{:S(2)}) %collective-permute-start.12) | collective-permute-done | bytes 1179680 | tf_op jit(solution)/shard_map/ppermute | solution.py:20
  322.2 4.4 fusion.7
  326.8 18.7 %collective-permute-done.6 = bf16[2,1,1152,1,2,2,128]{2,6,0,5,4,3,1:T(8,128)(2,1)} collective-permute-done((bf16[2,1,1152,1,2,2,128]{2,6,0,5,4,3,1:T(8,128)(2,1)S(1)}, bf16[2,1,1152,1,2,2,128]{2,6,0,5,4,3,1:T(8,128)(2,1)}, u32[]{:S(2)}, u32[]{:S(2)}) %collective-permute-start.6) | collective-permute-done | bytes 2359328 | tf_op jit(solution)/shard_map/ppermute | solution.py:20
  345.6 4.0 fusion.3
  358.5 18.7 %all-to-all-start.1 = ((bf16[1,32,36,896]{3,2,0,1:T(8,128)(2,1)}), bf16[1,32,36,896]{3,2,0,1:T(8,128)(2,1)S(1)}, u32[]{:S(2)}, u32[]{:S(2)}) async-start(bf16[1,32,36,896]{3,2,0,1:T(8,128)(2,1)} %bitcast.146), calls=%async_computation.1 | async-start | bytes 4587520 | tf_op jit(solution)/shard_map/all_to_all | solution.py:143
  377.2 31.2 %collective-permute-done.13 = bf16[2,1,1152,1,2,2,128]{2,6,0,5,4,3,1:T(8,128)(2,1)} collective-permute-done((bf16[2,1,1152,1,2,2,128]{2,6,0,5,4,3,1:T(8,128)(2,1)}, bf16[2,1,1152,1,2,2,128]{2,6,0,5,4,3,1:T(8,128)(2,1)}, u32[]{:S(2)}, u32[]{:S(2)}) %collective-permute-start.13) | collective-permute-done | bytes 2359328 | tf_op jit(solution)/shard_map/ppermute | solution.py:20
  408.4 4.3 fusion.1
  416.9 4.1 fusion.5
  421.0 3.9 reshape.1137
  425.0 24.9 %all-to-all-done.1 = bf16[1,32,36,896]{3,2,0,1:T(8,128)(2,1)S(1)} async-done(((bf16[1,32,36,896]{3,2,0,1:T(8,128)(2,1)}), bf16[1,32,36,896]{3,2,0,1:T(8,128)(2,1)S(1)}, u32[]{:S(2)}, u32[]{:S(2)}) %all-to-all-start.1) | async-done | bytes 2064416 | tf_op jit(solution)/shard_map/all_to_all | solution.py:143
  449.9 10.8 %all-to-all-start.3 = ((bf16[1,32,36,896]{3,2,0,1:T(8,128)(2,1)}), bf16[1,32,36,896]{3,2,0,1:T(8,128)(2,1)}, u32[]{:S(2)}, u32[]{:S(2)}) async-start(bf16[1,32,36,896]{3,2,0,1:T(8,128)(2,1)} %bitcast.145), calls=%async_computation.3 | async-start | bytes 4587520 | tf_op jit(solution)/shard_map/all_to_all | solution.py:143
  464.3 13.4 %gather_fusion.1 = bf16[1024,896]{1,0:T(8,128)(2,1)} fusion(bf16[1,1152,896]{2,1,0:T(8,128)(2,1)S(1)} %reshape.1128, s32[1024]{0:T(1024)S(1)} %bitcast.142), kind=kCustom, calls=%fused_computation.1.clone | custom fusion | bytes 3678208 | tf_op jit(solution)/shard_map/vmap(jit(_take))/gather | solution.py:33
  482.6 33.7 %all-to-all-done.3 = bf16[1,32,36,896]{3,2,0,1:T(8,128)(2,1)} async-done(((bf16[1,32,36,896]{3,2,0,1:T(8,128)(2,1)}), bf16[1,32,36,896]{3,2,0,1:T(8,128)(2,1)}, u32[]{:S(2)}, u32[]{:S(2)}) %all-to-all-start.3) | async-done | bytes 2064416 | tf_op jit(solution)/shard_map/all_to_all | solution.py:143
  518.8 13.4 %gather_fusion.3 = bf16[1024,896]{1,0:T(8,128)(2,1)} fusion(bf16[1,1152,896]{2,1,0:T(8,128)(2,1)S(1)} %reshape.1138, s32[1024]{0:T(1024)S(1)} %bitcast.141), kind=kCustom, calls=%fused_computation.3.clone | custom fusion | bytes 3678208 | tf_op jit(solution)/shard_map/vmap(jit(_take))/gather | solution.py:33
  (181 shorter events, 97.0 us)
Async XLA Ops:
  0.0 145.3 %copy-start = (bf16[1,1,1024,896]{3,2,1,0:T(8,128)(2,1)S(1)}, bf16[1,1,1024,896]{3,2,1,0:T(8,128)(2,1)}, u32[]{:S(2)}) copy-start(bf16[1,1,1024,896]{3,2,1,0:T(8,128)(2,1)} %param.21) | copy-start | bytes 5505028
  0.0 7.0 %copy-start.20 = (s32[1,2,1,64]{3,2,1,0:T(1,128)S(1)}, s32[1,2,1,64]{3,2,1,0:T(1,128)}, u32[]{:S(2)}) copy-start(s32[1,2,1,64]{3,2,1,0:T(1,128)} %param.15) | copy-start | bytes 1540
  0.0 8.7 %copy-start.19 = (f32[1,2,64,2]{2,3,1,0:T(2,128)S(1)}, f32[1,2,64,2]{2,3,1,0:T(2,128)}, u32[]{:S(2)}) copy-start(f32[1,2,64,2]{2,3,1,0:T(2,128)} %param.16) | copy-start | bytes 3076
  2.6 23.3 %collective-permute-start = (bf16[64,7168]{1,0:T(8,128)(2,1)S(1)}, bf16[64,7168]{1,0:T(8,128)(2,1)}, u32[]{:S(2)}, u32[]{:S(2)}) collective-permute-start(bf16[64,7168]{1,0:T(8,128)(2,1)S(1)} %get-tuple-element.17), channel_id=1, source_target_pairs={{0,224},{32,0},{64,32},{96,64},{128,96},{160,128},{192,160},{224,1... | collective-permute-start | bytes 2752520 | tf_op jit(solution)/shard_map/ppermute | solution.py:14
  8.1 32.9 %copy-start.16 = (s32[64,2]{1,0:T(8,128)}, s32[64,2]{1,0:T(8,128)S(1)}, u32[]{:S(2)}) copy-start(s32[64,2]{1,0:T(8,128)S(1)} %copy.80) | copy-start | bytes 1540
  48.0 11.4 %copy-start.12 = (bf16[64,7168]{1,0:T(8,128)(2,1)S(1)}, bf16[64,7168]{1,0:T(8,128)(2,1)}, u32[]{:S(2)}) copy-start(bf16[64,7168]{1,0:T(8,128)(2,1)} %get-tuple-element.18) | copy-start | bytes 2752516
  48.0 80.2 %all-to-all-start = ((bf16[1,32,36,896]{3,2,0,1:T(8,128)(2,1)}), bf16[1,32,36,896]{3,2,0,1:T(8,128)(2,1)}, u32[]{:S(2)}, u32[]{:S(2)}) async-start(bf16[1,32,36,896]{3,2,0,1:T(8,128)(2,1)} %bitcast.144), calls=%async_computation | async-start | bytes 4587520 | tf_op jit(solution)/shard_map/all_to_all | solution.py:138
  59.5 46.6 %collective-permute-start.7 = (bf16[64,7168]{1,0:T(8,128)(2,1)S(1)}, bf16[64,7168]{1,0:T(8,128)(2,1)}, u32[]{:S(2)}, u32[]{:S(2)}) collective-permute-start(bf16[64,7168]{1,0:T(8,128)(2,1)S(1)} %copy-done.12), channel_id=1, source_target_pairs={{0,32},{32,64},{64,96},{96,128},{128,160},{160,192},{192,224},{224... | collective-permute-start | bytes 2752520 | tf_op jit(solution)/shard_map/ppermute | solution.py:14
  128.3 68.6 %all-to-all-start.2 = ((bf16[1,32,36,896]{3,2,0,1:T(8,128)(2,1)}), bf16[1,32,36,896]{3,2,0,1:T(8,128)(2,1)}, u32[]{:S(2)}, u32[]{:S(2)}) async-start(bf16[1,32,36,896]{3,2,0,1:T(8,128)(2,1)} %bitcast.143), calls=%async_computation.2 | async-start | bytes 4587520 | tf_op jit(solution)/shard_map/all_to_all | solution.py:138
  152.1 65.5 %collective-permute-start.1 = (bf16[1,1152,1,2,2,128]{1,5,4,3,2,0:T(8,128)(2,1)S(1)}, bf16[1,1152,1,2,2,128]{1,5,4,3,2,0:T(8,128)(2,1)}, u32[]{:S(2)}, u32[]{:S(2)}) collective-permute-start(bf16[1,1152,1,2,2,128]{1,5,4,3,2,0:T(8,128)(2,1)S(1)} %fusion.24), channel_id=1, source_target_pairs={{0,4},{1,5},{2,6},{3,7},{4,0},{5,1},{6,2},{7,3},{8,12},{9,13},{10,... | collective-permute-start | bytes 3538952 | tf_op jit(solution)/shard_map/ppermute | solution.py:20
  200.8 16.8 %copy-start.7 = (f32[1152,2,2,2,128]{0,4,3,2,1:T(8,128)S(1)}, f32[1152,2,2,2,128]{0,4,3,2,1:T(8,128)}, u32[]{:S(2)}) copy-start(f32[1152,2,2,2,128]{0,4,3,2,1:T(8,128)} %copy-done.6) | copy-start | bytes 14155780
  205.4 15.0 %copy-start.5 = (f32[1152,2,2,2,128]{0,4,3,2,1:T(8,128)}, f32[1152,2,2,2,128]{0,4,3,2,1:T(8,128)S(1)}, u32[]{:S(2)}) copy-start(f32[1152,2,2,2,128]{0,4,3,2,1:T(8,128)S(1)} %fusion.10) | copy-start | bytes 14155780
  220.1 14.3 %collective-permute-start.2 = (bf16[1,1152,1,1,2,128]{1,5,4,3,2,0:T(8,128)(2,1)}, bf16[1,1152,1,1,2,128]{1,5,4,3,2,0:T(8,128)(2,1)}, u32[]{:S(2)}, u32[]{:S(2)}) collective-permute-start(bf16[1,1152,1,1,2,128]{1,5,4,3,2,0:T(8,128)(2,1)} %dynamic-slice_convert_fusion.3), channel_id=1, source_target_pairs={{0,2},{1,3},{2,0},{3,1},{4,6},{5,7},{6,4},{7,5},{8,10},{9,11},{10,... | collective-permute-start | bytes 1769480 | tf_op jit(solution)/shard_map/ppermute | solution.py:20
  221.5 26.6 %collective-permute-start.8 = (bf16[1,1152,1,2,2,128]{1,5,4,3,2,0:T(8,128)(2,1)}, bf16[1,1152,1,2,2,128]{1,5,4,3,2,0:T(8,128)(2,1)}, u32[]{:S(2)}, u32[]{:S(2)}) collective-permute-start(bf16[1,1152,1,2,2,128]{1,5,4,3,2,0:T(8,128)(2,1)} %fusion.25), channel_id=1, source_target_pairs={{0,4},{1,5},{2,6},{3,7},{4,0},{5,1},{6,2},{7,3},{8,12},{9,13},{10,... | collective-permute-start | bytes 3538952 | tf_op jit(solution)/shard_map/ppermute | solution.py:20
  235.6 16.9 %copy-start.11 = (f32[1,1,1152,128]{2,3,1,0:T(8,128)S(1)}, f32[1,1,1152,128]{2,3,1,0:T(8,128)}, u32[]{:S(2)}) copy-start(f32[1,1,1152,128]{2,3,1,0:T(8,128)} %copy.75) | copy-start | bytes 1769476
  235.6 16.9 %collective-permute-start.3 = (bf16[1,1152,1,1,1,128]{1,5,4,3,2,0:T(8,128)(2,1)S(1)}, bf16[1,1152,1,1,1,128]{1,5,4,3,2,0:T(8,128)(2,1)S(1)}, u32[]{:S(2)}, u32[]{:S(2)}) collective-permute-start(bf16[1,1152,1,1,1,128]{1,5,4,3,2,0:T(8,128)(2,1)S(1)} %dynamic-slice_convert_fusion.5), channel_id=1, source_target_pairs={{0,1},{1,0},{2,3},{3,2},{4,5},{5,4},{6,7},{7,6},{8,9},{9,8},{10,11... | collective-permute-start | bytes 884744 | tf_op jit(solution)/shard_map/ppermute | solution.py:20
  251.2 13.1 %collective-permute-start.9 = (bf16[1,1152,1,1,2,128]{1,5,4,3,2,0:T(8,128)(2,1)}, bf16[1,1152,1,1,2,128]{1,5,4,3,2,0:T(8,128)(2,1)}, u32[]{:S(2)}, u32[]{:S(2)}) collective-permute-start(bf16[1,1152,1,1,2,128]{1,5,4,3,2,0:T(8,128)(2,1)} %dynamic-slice_convert_fusion.2), channel_id=1, source_target_pairs={{0,2},{1,3},{2,0},{3,1},{4,6},{5,7},{6,4},{7,5},{8,10},{9,11},{10,... | collective-permute-start | bytes 1769480 | tf_op jit(solution)/shard_map/ppermute | solution.py:20
  252.9 12.6 %copy-start.10 = (bf16[2,1,1152,1,1,1,128]{2,6,0,5,4,3,1:T(8,128)(2,1)}, bf16[2,1,1152,1,1,1,128]{2,6,0,5,4,3,1:T(8,128)(2,1)S(1)}, u32[]{:S(2)}) copy-start(bf16[2,1,1152,1,1,1,128]{2,6,0,5,4,3,1:T(8,128)(2,1)S(1)} %maximum_bitcast_fusion.1) | copy-start | bytes 1769476
  252.9 12.6 %collective-permute-start.4 = (bf16[2,1,1152,1,1,1,128]{2,6,0,5,4,3,1:T(8,128)(2,1)S(1)}, bf16[2,1,1152,1,1,1,128]{2,6,0,5,4,3,1:T(8,128)(2,1)}, u32[]{:S(2)}, u32[]{:S(2)}) collective-permute-start(bf16[2,1,1152,1,1,1,128]{2,6,0,5,4,3,1:T(8,128)(2,1)S(1)} %maximum_bitcast_fusion.1), channel_id=1, source_target_pairs={{0,1},{1,0},{2,3},{3,2},{4,5},{5,4},{6,7},{7,6},{8,9},{9,8},{10,11... | collective-permute-start | bytes 1769480 | tf_op jit(solution)/shard_map/ppermute | solution.py:20
  265.5 7.9 %copy-start.8 = (f32[1,1,1,32,36,128]{5,3,4,2,1,0:T(8,128)S(1)}, f32[1,1,1,32,36,128]{5,3,4,2,1,0:T(8,128)}, u32[]{:S(2)}) copy-start(f32[1,1,1,32,36,128]{5,3,4,2,1,0:T(8,128)} %get-tuple-element.20) | copy-start | bytes 1769476
  268.1 7.2 %copy-start.9 = (f32[1,1,1,32,36,128]{5,3,4,2,1,0:T(8,128)S(1)}, f32[1,1,1,32,36,128]{5,3,4,2,1,0:T(8,128)}, u32[]{:S(2)}) copy-start(f32[1,1,1,32,36,128]{5,3,4,2,1,0:T(8,128)} %get-tuple-element.22) | copy-start | bytes 1769476
  268.1 25.1 %collective-permute-start.5 = (bf16[2,1,1152,1,1,2,128]{2,6,0,5,4,3,1:T(8,128)(2,1)S(1)}, bf16[2,1,1152,1,1,2,128]{2,6,0,5,4,3,1:T(8,128)(2,1)}, u32[]{:S(2)}, u32[]{:S(2)}) collective-permute-start(bf16[2,1,1152,1,1,2,128]{2,6,0,5,4,3,1:T(8,128)(2,1)S(1)} %fusion.23), channel_id=1, source_target_pairs={{0,2},{1,3},{2,0},{3,1},{4,6},{5,7},{6,4},{7,5},{8,10},{9,11},{10,... | collective-permute-start | bytes 3538952 | tf_op jit(solution)/shard_map/ppermute | solution.py:20
  270.4 6.2 %collective-permute-start.10 = (bf16[1,1152,1,1,1,128]{1,5,4,3,2,0:T(8,128)(2,1)}, bf16[1,1152,1,1,1,128]{1,5,4,3,2,0:T(8,128)(2,1)}, u32[]{:S(2)}, u32[]{:S(2)}) collective-permute-start(bf16[1,1152,1,1,1,128]{1,5,4,3,2,0:T(8,128)(2,1)} %dynamic-slice_convert_fusion.4), channel_id=1, source_target_pairs={{0,1},{1,0},{2,3},{3,2},{4,5},{5,4},{6,7},{7,6},{8,9},{9,8},{10,11... | collective-permute-start | bytes 884744 | tf_op jit(solution)/shard_map/ppermute | solution.py:20
  278.1 19.4 %collective-permute-start.11 = (bf16[2,1,1152,1,1,1,128]{2,6,0,5,4,3,1:T(8,128)(2,1)S(1)}, bf16[2,1,1152,1,1,1,128]{2,6,0,5,4,3,1:T(8,128)(2,1)S(1)}, u32[]{:S(2)}, u32[]{:S(2)}) collective-permute-start(bf16[2,1,1152,1,1,1,128]{2,6,0,5,4,3,1:T(8,128)(2,1)S(1)} %maximum_bitcast_fusion.2), channel_id=1, source_target_pairs={{0,1},{1,0},{2,3},{3,2},{4,5},{5,4},{6,7},{7,6},{8,9},{9,8},{10,11... | collective-permute-start | bytes 1769480 | tf_op jit(solution)/shard_map/ppermute | solution.py:20
  296.2 49.3 %collective-permute-start.6 = (bf16[2,1,1152,1,2,2,128]{2,6,0,5,4,3,1:T(8,128)(2,1)S(1)}, bf16[2,1,1152,1,2,2,128]{2,6,0,5,4,3,1:T(8,128)(2,1)}, u32[]{:S(2)}, u32[]{:S(2)}) collective-permute-start(bf16[2,1,1152,1,2,2,128]{2,6,0,5,4,3,1:T(8,128)(2,1)S(1)} %fusion.9), channel_id=1, source_target_pairs={{0,4},{1,5},{2,6},{3,7},{4,0},{5,1},{6,2},{7,3},{8,12},{9,13},{10,... | collective-permute-start | bytes 7077896 | tf_op jit(solution)/shard_map/ppermute | solution.py:20
  298.2 24.1 %collective-permute-start.12 = (bf16[2,1,1152,1,1,2,128]{2,6,0,5,4,3,1:T(8,128)(2,1)S(1)}, bf16[2,1,1152,1,1,2,128]{2,6,0,5,4,3,1:T(8,128)(2,1)}, u32[]{:S(2)}, u32[]{:S(2)}) collective-permute-start(bf16[2,1,1152,1,1,2,128]{2,6,0,5,4,3,1:T(8,128)(2,1)S(1)} %fusion.21), channel_id=1, source_target_pairs={{0,2},{1,3},{2,0},{3,1},{4,6},{5,7},{6,4},{7,5},{8,10},{9,11},{10,... | collective-permute-start | bytes 3538952 | tf_op jit(solution)/shard_map/ppermute | solution.py:20
  326.6 81.8 %collective-permute-start.13 = (bf16[2,1,1152,1,2,2,128]{2,6,0,5,4,3,1:T(8,128)(2,1)}, bf16[2,1,1152,1,2,2,128]{2,6,0,5,4,3,1:T(8,128)(2,1)}, u32[]{:S(2)}, u32[]{:S(2)}) collective-permute-start(bf16[2,1,1152,1,2,2,128]{2,6,0,5,4,3,1:T(8,128)(2,1)} %fusion.7), channel_id=1, source_target_pairs={{0,4},{1,5},{2,6},{3,7},{4,0},{5,1},{6,2},{7,3},{8,12},{9,13},{10,... | collective-permute-start | bytes 7077896 | tf_op jit(solution)/shard_map/ppermute | solution.py:20
  358.5 91.4 %all-to-all-start.1 = ((bf16[1,32,36,896]{3,2,0,1:T(8,128)(2,1)}), bf16[1,32,36,896]{3,2,0,1:T(8,128)(2,1)S(1)}, u32[]{:S(2)}, u32[]{:S(2)}) async-start(bf16[1,32,36,896]{3,2,0,1:T(8,128)(2,1)} %bitcast.146), calls=%async_computation.1 | async-start | bytes 4587520 | tf_op jit(solution)/shard_map/all_to_all | solution.py:143
  449.9 11.8 %copy-start.2 = (bf16[1,32,36,896]{3,2,0,1:T(8,128)(2,1)}, bf16[1,32,36,896]{3,2,0,1:T(8,128)(2,1)S(1)}, u32[]{:S(2)}) copy-start(bf16[1,32,36,896]{3,2,0,1:T(8,128)(2,1)S(1)} %all-to-all-done.1) | copy-start | bytes 6193156
  449.9 10.9 %copy-start.15 = (s32[64,2]{1,0:T(8,128)S(1)}, s32[64,2]{1,0:T(8,128)}, u32[]{:S(2)}) copy-start(s32[64,2]{1,0:T(8,128)} %copy-done.14) | copy-start | bytes 1540
  449.9 11.3 %copy-start.17 = (s32[64,2]{1,0:T(8,128)S(1)}, s32[64,2]{1,0:T(8,128)}, u32[]{:S(2)}) copy-start(s32[64,2]{1,0:T(8,128)} %copy-done.16) | copy-start | bytes 1540
  449.9 66.4 %all-to-all-start.3 = ((bf16[1,32,36,896]{3,2,0,1:T(8,128)(2,1)}), bf16[1,32,36,896]{3,2,0,1:T(8,128)(2,1)}, u32[]{:S(2)}, u32[]{:S(2)}) async-start(bf16[1,32,36,896]{3,2,0,1:T(8,128)(2,1)} %bitcast.145), calls=%async_computation.3 | async-start | bytes 4587520 | tf_op jit(solution)/shard_map/all_to_all | solution.py:143
  (11 other events, 33.8 us)
where the time goes:
time: 550 us; the launch traced here: 541 us
  waiting for transfers between devices  289 us (53%)
  local copies, waits for them, and re-layouts  108 us (20%)
  starting transfers between devices  74.3 us (14%)
  other arithmetic  46.9 us (9%)
  matrix products  21.2 us (4%)
    ppermute x12, waiting for transfers between devices, partner_2(): return lax.ppermute(value, axis, pairs)  127 us
    all_to_all x4, waiting for transfers between devices, local(): lax.all_to_all(payload, 'ep', split_axis=1, concat_axis=1, tiled=True)  102 us
    ppermute x2, waiting for transfers between devices, passed_along(): return lax.ppermute(value, axis, pairs)  59.9 us
    all_to_all x4, starting transfers between devices, local(): lax.all_to_all(payload, 'ep', split_axis=1, concat_axis=1, tiled=True)  53.9 us
    gather x8, local copies, waits for them, and re-layouts, take_rows(): return jnp.take(source, indices, axis=0)  53.8 us
    concatenate x6, other arithmetic, gather_parts(): triple = jnp.concatenate([partner, current, partner], axis=split_axis)  18.9 us
    ppermute x12, starting transfers between devices, partner_2(): return lax.ppermute(value, axis, pairs)  13.8 us
  transfers between devices with their start and end apart: 18, of which 13 were waited for; matrix products, arithmetic and copies ran while one was open for 22% of the time, Pallas kernels for 0%

commit v1 on v0

v1 whole, which is shorter than its diff:
```python
import functools

import jax
import jax.numpy as jnp
from jax import lax
from jax.experimental import pallas as pl
from jax.experimental.pallas import tpu as pltpu
from jax.sharding import PartitionSpec as P

MESH = pl.DeviceIdType.MESH
BF = jnp.bfloat16
F32 = jnp.float32
CAP = 36
TOK = 64
SL = 896
FF = 1024
CH = 4 * CAP
NCH = 16
NT = (((1,), (1,)), ((), ()))

ORDER = (
    ("disp", 0),
    ("core", 6),
    ("xhop", 5),
    ("exp", 3),
    ("act", 4),
    ("sum", 3),
    ("out", 6),
)


def kernel(
    meta, handed, gate, up, w1, w3, w2, out,
    A, DS, R, PB, RS1, SZS, SZR, OWN, H, ES, B, OS, MR, T, TT, OH, RP, OHT, W1P, W3P, W2P, GV, UV,
    w_sem, gu_sem, m_s, m_r, a_s, a_r, ds_s, r_r, rs_s, rs_r, sz_s, sz_r, hz_s, hz_r,
    hx_s, hx_r, hc_s, hc_r, es_s, b_r, o_s, o_r, ol_s,
):
    s = lax.axis_index("section")
    ep = lax.axis_index("ep")
    z = ep // 4
    xl = (ep // 2) % 2
    c = ep % 2
    pid = ep % 4
    e = z // 2
    zp = z % 2
    pos2 = c * 2 + xl
    pos = pos2 * 2 + zp
    after = (s + 1) % 8
    before = (s + 7) % 8
    zpart = (z + 1 - 2 * zp) * 4 + pid
    xpart = z * 4 + (1 - xl) * 2 + c
    cpart = z * 4 + xl * 2 + 1 - c

    def rcopy(src, dst, ssem, rsem, epi, sec=None):
        return pltpu.make_async_remote_copy(
            src_ref=src, dst_ref=dst, send_sem=ssem, recv_sem=rsem,
            device_id={"section": s if sec is None else sec, "ep": epi}, device_id_type=MESH,
        )

    def lanes(start, size):
        return pl.ds(pl.multiple_of(start, 128), size)

    loads = []
    for p in range(8):
        j = (p & 1) * 4 + ((p >> 1) & 1) * 2 + (p >> 2)
        here, there = pl.ds(p * 128, 128), pl.ds(j * 128, 128)
        loads.append(pltpu.make_async_copy(w2.at[there, :], W2P.at[here, :], w_sem.at[p]))
        loads.append(pltpu.make_async_copy(w1.at[:, there], W1P.at[:, here], w_sem.at[8 + p]))
        loads.append(pltpu.make_async_copy(w3.at[:, there], W3P.at[:, here], w_sem.at[16 + p]))
    loads.append(pltpu.make_async_copy(gate, GV, gu_sem.at[0]))
    loads.append(pltpu.make_async_copy(up, UV, gu_sem.at[1]))

    bar = pltpu.get_barrier_semaphore()

    def greet(sec, epi):
        pl.semaphore_signal(bar, inc=1, device_id={"section": sec, "ep": epi}, device_id_type=MESH)

    for k in range(4):
        greet(after, z * 4 + k)
        greet(before, z * 4 + k)
    for k in range(1, 4):
        greet(s, z * 4 + (pid + k) % 4)
    for k in range(1, 8):
        greet(s, ((z + k) % 8) * 4 + pid)
    pl.semaphore_wait(bar, 18)

    def meta_copy(k):
        other = (pid + k) % 4
        return rcopy(meta, MR.at[pl.ds(pid * 16, 16), :], m_s.at[k], m_r.at[pid], z * 4 + other)

    for k in range(1, 4):
        meta_copy(k).start()

    def relay(d, turn, k):
        q = zp if turn == 0 else 1 - zp
        other = (pid + k) % 4
        return rcopy(
            handed.at[d, :, lanes((q * 4 + other) * SL, SL)],
            A.at[d, q, pl.ds(pl.multiple_of(pid * TOK, TOK), TOK), :],
            a_s.at[(d * 2 + turn) * 4 + k],
            a_r.at[(d * 2 + turn) * 4 + pid],
            z * 4 + other,
            before if d == 0 else after,
        )

    for d in range(2):
        for turn in range(2):
            for k in range(4):
                relay(d, turn, k).start()
    for load in loads:
        load.start()

    MR[pl.ds(pl.multiple_of(pid * 16, 16), 16), :] = meta[...]
    for k in range(1, 4):
        other = (pid + k) % 4
        rcopy(meta, MR.at[pl.ds(other * 16, 16), :], m_s.at[k], m_r.at[other], zpart).wait_recv()
    rows = MR[...]
    cols = jnp.concatenate([rows, rows], axis=0).T
    lane = lax.broadcasted_iota(jnp.int32, (TOK, 128), 1)
    for src in range(4):
        acc = jnp.zeros((TOK, 128), F32)
        for d in range(2):
            base = src * 16 + d * 8
            r_e0, r_e1, r_ord = (rows[base + f : base + f + 1, :] for f in range(3))
            c_ord = cols[:TOK, base + 2 : base + 3]
            for k in range(2):
                c_e = cols[:TOK, base + k : base + k + 1]
                earlier = (r_ord < c_ord) & ((r_e0 == c_e) | (r_e1 == c_e)) & (lane < TOK)
                count = jnp.sum(jnp.where(earlier, 1.0, 0.0), axis=1, keepdims=True)
                target = c_e * float(CH) + float(src * CAP) + count
                acc = jnp.where(lane == d * 2 + k, target, acc)
                prob = cols[:TOK, base + 3 + k : base + 4 + k]
                acc = jnp.where(lane == 4 + d * 2 + k, prob, acc)
        T[src * TOK : (src + 1) * TOK, :] = acc
    TT[...] = T[...].T
    for d in range(2):
        row0, row1 = TT[d * 2 : d * 2 + 1, :], TT[d * 2 + 1 : d * 2 + 2, :]
        p0, p1 = TT[4 + d * 2 : 5 + d * 2, :], TT[5 + d * 2 : 6 + d * 2, :]
        for ex in range(4):
            ids = (lax.broadcasted_iota(jnp.int32, (CH, 256), 0) + ex * CH).astype(F32)
            hit0, hit1 = ids == row0, ids == row1
            OH[d * 4 + ex] = jnp.where(hit0 | hit1, 1.0, 0.0).astype(BF)
            scale = jnp.sum(
                jnp.where(hit0, p0, 0.0) + jnp.where(hit1, p1, 0.0), axis=1, keepdims=True
            )
            RP[d * 4 + ex] = jnp.broadcast_to(scale, (CH, 128))
        ids = lax.broadcasted_iota(jnp.int32, (256, 4 * CH), 1).astype(F32)
        hit = (ids == T[:, d * 2 : d * 2 + 1]) | (ids == T[:, d * 2 + 1 : d * 2 + 2])
        OHT[d] = jnp.where(hit, 1.0, 0.0).astype(BF)

    def offset(i):
        half = (i + 1) // 2
        return jnp.where(i % 2 == 1, half, 8 - half)

    def source(n):
        d = n // 8
        return d, (2 * e + offset(n % 8)) % 8

    def wait_relay(d, turn):
        q = zp if turn == 0 else 1 - zp
        for k in range(4):
            rcopy(
                A.at[d, q, pl.ds(k * TOK, TOK), :], A.at[d, q, pl.ds(k * TOK, TOK), :],
                a_s.at[0], a_r.at[(d * 2 + turn) * 4 + k], zpart,
            ).wait_recv()

    def disp(n):
        for d_ in range(2):
            for turn in range(2):
                @pl.when(n == d_ * 8 + turn)
                def _():
                    wait_relay(d_, turn)

        d, m = n // 8, n % 8
        zd = (z + offset(m)) % 8
        ed, qd = zd // 2, zd % 2
        picked = jnp.dot(OH[d * 4 + ed], A[d, qd], preferred_element_type=F32)
        scaled = (picked * RP[d * 4 + ed][:, 0:1]).astype(BF)

        @pl.when(m == 0)
        def _():
            R[d * 8 + z] = scaled

        @pl.when(m != 0)
        def _():
            DS[d * 8 + zd] = scaled
            rcopy(
                DS.at[d * 8 + zd], R.at[d * 8 + z], ds_s.at[d * 8 + zd], r_r.at[d * 8 + z],
                zd * 4 + pid,
            ).start()

    def partial(q, k):
        other = (pid + k) % 4
        wide = lanes(((other % 2) * 2 + other // 2) * 256, 256)
        return rcopy(
            PB.at[q, :, wide], RS1.at[q, pid], rs_s.at[q * 4 + k], rs_r.at[q * 4 + pid],
            z * 4 + other,
        )

    def exp(n):
        d, zs = source(n)
        q = d * 8 + zs

        @pl.when(zs != z)
        def _():
            rcopy(R.at[q], R.at[q], ds_s.at[q], r_r.at[q], zpart).wait_recv()

        PB[q] = lax.dot_general(R[q], W2P[...], NT, preferred_element_type=F32).astype(BF)
        for k in range(1, 4):
            partial(q, k).start()

    def zsum(q):
        return rcopy(SZS.at[q], SZR.at[q], sz_s.at[q], sz_r.at[q], zpart)

    def sum_(n):
        d, zs = source(n)
        q = d * 8 + zs
        total = PB[q, :, lanes(pos2 * 256, 256)].astype(F32)
        for k in range(1, 4):
            other = (pid + k) % 4
            rcopy(
                RS1.at[q, other], RS1.at[q, other], rs_s.at[q * 4], rs_r.at[q * 4 + other], zpart
            ).wait_recv()
            total = total + RS1[q, other].astype(F32)
        low, high = total[:, :128], total[:, 128:]
        SZS[q] = jnp.where(zp == 0, high, low).astype(BF)
        OWN[q] = jnp.where(zp == 0, low, high)
        zsum(q).start()

    def grads(q, width, start, ssem, rsem, to):
        part = H.at[q, :, :, lanes(start, width)]
        return rcopy(part, part, ssem.at[q], rsem.at[q], to)

    def act(n):
        d, zs = source(n)
        q = d * 8 + zs
        zsum(q).wait_recv()
        grad = OWN[q] + SZR[q].astype(F32)
        g, u = GV[q].astype(F32), UV[q].astype(F32)
        sigma = jax.nn.sigmoid(g)
        here = lanes(pos * 128, 128)
        H[q, 0, :, here] = (grad * u * sigma * (1.0 + g * (1.0 - sigma))).astype(BF)
        H[q, 1, :, here] = (grad * g * sigma).astype(BF)
        grads(q, 128, pos * 128, hz_s, hz_r, zpart).start()

    def xhop(n):
        d, zs = source(n)
        q = d * 8 + zs
        grads(q, 128, (pos2 * 2 + 1 - zp) * 128, hz_s, hz_r, zpart).wait_recv()
        grads(q, 256, pos2 * 256, hx_s, hx_r, xpart).start()

    def core(n):
        d, zs = source(n)
        q = d * 8 + zs
        grads(q, 256, (c * 2 + 1 - xl) * 256, hx_s, hx_r, xpart).wait_recv()
        grads(q, 512, c * 512, hc_s, hc_r, cpart).start()

    def back(q, d, zs):
        return rcopy(ES.at[q], B.at[d, zp, e], es_s.at[q], b_r.at[d * 8 + z], zs * 4 + pid)

    def out_(n):
        d, zs = source(n)
        q = d * 8 + zs
        grads(q, 512, (1 - c) * 512, hc_s, hc_r, cpart).wait_recv()
        result = lax.dot_general(H[q, 0], W1P[...], NT, preferred_element_type=F32)
        result = result + lax.dot_general(H[q, 1], W3P[...], NT, preferred_element_type=F32)

        @pl.when(zs == z)
        def _():
            B[d, zp, e] = result.astype(BF)

        @pl.when(zs != z)
        def _():
            ES[q] = result.astype(BF)
            back(q, d, zs).start()

    def final(d, par, k):
        other = (pid + k) % 4
        return rcopy(
            OS.at[d, par, pl.ds(pl.multiple_of(other * TOK, TOK), TOK), :],
            out.at[d, :, lanes((par * 4 + pid) * SL, SL)],
            o_s.at[(d * 2 + par) * 4 + k], o_r.at[(d * 2 + par) * 4 + pid], z * 4 + other,
        )

    def final_own(d, par):
        return pltpu.make_async_copy(
            OS.at[d, par, pl.ds(pl.multiple_of(pid * TOK, TOK), TOK), :],
            out.at[d, :, lanes((par * 4 + pid) * SL, SL)],
            ol_s.at[d * 2 + par],
        )

    def combine(d):
        for par in range(2):
            for ex in range(4):
                zo = ex * 2 + par

                @pl.when(zo != z)
                def _():
                    rcopy(
                        B.at[d, par, ex], B.at[d, par, ex], es_s.at[0], b_r.at[d * 8 + zo], zpart
                    ).wait_recv()

            table = B[d, par].reshape(4 * CH, SL)
            OS[d, par] = jnp.dot(OHT[d], table, preferred_element_type=F32).astype(BF)
            for k in range(1, 4):
                final(d, par, k).start()
            final_own(d, par).start()

    for load in loads:
        load.wait()

    stages = {
        "disp": disp, "exp": exp, "sum": sum_, "act": act, "xhop": xhop, "core": core, "out": out_,
    }
    longest = max(lag for _, lag in ORDER)

    def step(t, carry):
        for name, lag in ORDER:
            n = t - lag

            @pl.when((n >= 0) & (n < NCH))
            def _():
                stages[name](jnp.clip(n, 0, NCH - 1))

        @pl.when(t == 8 + longest + 1)
        def _():
            combine(0)

        return carry

    lax.fori_loop(0, NCH + longest, step, 0)
    combine(1)

    for d in range(2):
        for par in range(2):
            final_own(d, par).wait()
            for k in range(1, 4):
                other = (pid + k) % 4
                rcopy(
                    out.at[d, :, lanes((par * 4 + other) * SL, SL)],
                    out.at[d, :, lanes((par * 4 + other) * SL, SL)],
                    o_s.at[0], o_r.at[(d * 2 + par) * 4 + other], zpart,
                ).wait_recv()
                final(d, par, k).wait_send()
            for k in range(4):
                relay(d, par, k).wait_send()
    for k in range(1, 4):
        meta_copy(k).wait_send()

    def drain(n, carry):
        d, zs = source(n)
        q = d * 8 + zs
        for k in range(1, 4):
            partial(q, k).wait_send()
        zsum(q).wait_send()
        grads(q, 128, pos * 128, hz_s, hz_r, zpart).wait_send()
        grads(q, 256, pos2 * 256, hx_s, hx_r, xpart).wait_send()
        grads(q, 512, c * 512, hc_s, hc_r, cpart).wait_send()

        @pl.when(zs != z)
        def _():
            rcopy(DS.at[q], R.at[d * 8 + z], ds_s.at[q], r_r.at[d * 8 + z], zpart).wait_send()
            back(q, d, zs).wait_send()

        return carry

    lax.fori_loop(0, NCH, drain, 0)


def local(handed, routes, slot_order, gate_probs, saved_gate, saved_up, w_gate, w_up, w_down):
    fields = jnp.concatenate(
        [
            routes[0].transpose(0, 2, 1).astype(F32),
            slot_order[0].astype(F32),
            gate_probs[0].transpose(0, 2, 1),
        ],
        axis=1,
    )
    meta = jnp.pad(fields, ((0, 0), (0, 3), (0, 128 - TOK))).reshape(16, 128)
    gate = saved_gate.reshape(NCH, CH, 128)
    up = saved_up.reshape(NCH, CH, 128)
    anyspace = pl.BlockSpec(memory_space=pl.ANY)
    dma = pltpu.SemaphoreType.DMA
    result = pl.pallas_call(
        kernel,
        out_shape=jax.ShapeDtypeStruct((2, TOK, 8 * SL), BF),
        in_specs=[pl.BlockSpec(memory_space=pltpu.VMEM)] + [anyspace] * 6,
        out_specs=anyspace,
        scratch_shapes=[
            pltpu.VMEM((2, 2, 256, SL), BF),
            pltpu.VMEM((NCH, CH, SL), BF),
            pltpu.VMEM((NCH, CH, SL), BF),
            pltpu.VMEM((NCH, CH, FF), BF),
            pltpu.VMEM((NCH, 4, CH, 256), BF),
            pltpu.VMEM((NCH, CH, 128), BF),
            pltpu.VMEM((NCH, CH, 128), BF),
            pltpu.VMEM((NCH, CH, 128), F32),
            pltpu.VMEM((NCH, 2, CH, FF), BF),
            pltpu.VMEM((NCH, CH, SL), BF),
            pltpu.VMEM((2, 2, 4, CH, SL), BF),
            pltpu.VMEM((2, 2, 256, SL), BF),
            pltpu.VMEM((64, 128), F32),
            pltpu.VMEM((256, 128), F32),
            pltpu.VMEM((128, 256), F32),
            pltpu.VMEM((8, CH, 256), BF),
            pltpu.VMEM((8, CH, 128), F32),
            pltpu.VMEM((2, 256, 4 * CH), BF),
            pltpu.VMEM((SL, FF), BF),
            pltpu.VMEM((SL, FF), BF),
            pltpu.VMEM((FF, SL), BF),
            pltpu.VMEM((NCH, CH, 128), BF),
            pltpu.VMEM((NCH, CH, 128), BF),
            dma((24,)), dma((2,)),
            dma((4,)), dma((4,)),
            dma((16,)), dma((16,)),
            dma((NCH,)), dma((NCH,)),
            dma((4 * NCH,)), dma((4 * NCH,)),
            dma((NCH,)), dma((NCH,)),
            dma((NCH,)), dma((NCH,)),
            dma((NCH,)), dma((NCH,)),
            dma((NCH,)), dma((NCH,)),
            dma((NCH,)), dma((NCH,)),
            dma((16,)), dma((16,)),
            dma((4,)),
        ],
        compiler_params=pltpu.CompilerParams(
            collective_id=0, has_side_effects=True, vmem_limit_bytes=62 * 1024 * 1024
        ),
    )(meta, handed[0], gate, up, w_gate[0, 0], w_up[0, 0], w_down[0, 0])
    return result[None]


def solution(mesh):
    in_specs = (
        P("section", None, "ep", None),
        P("section", None, "ep", None),
        P("section", None, "ep", None),
        P("section", None, "ep", None),
        P("section", None, "ep", None, None, None),
        P("section", None, "ep", None, None, None),
        P("section", "ep", None, None),
        P("section", "ep", None, None),
        P("section", "ep", None, None),
    )
    out_specs = P("section", None, "ep", None)
    return jax.shard_map(local, mesh=mesh, in_specs=in_specs, out_specs=out_specs, check_vma=False)
```

time: 550 us -> 342 us (0.62)
  the two profiles are of different devices: /device:TPU:3 before, /device:TPU:129 now
where the time goes in v1:
time: 342 us
  Pallas kernels  333 us (97%)
  local copies, waits for them, and re-layouts  6.28 us (2%)
    pallas_call x1, Pallas kernels, local(): pl.pallas_call(kernel, out_shape=jax.ShapeDtypeStruct((2, TOK, 8 * SL), B...  333 us

profile of v1, /device:TPU:129, one launch (start us, length us, event | category | flops | bytes accessed | tf_op | source)
XLA Modules:
  0.0 342.0 jit_solution(6483884584488090718)
XLA Ops:
  0.0 0.0 copy-start
  0.0 0.7 convert_bitcast_fusion.1
  0.7 0.7 convert_bitcast_fusion
  1.4 1.3 fusion.meta
  2.7 1.3 copy.14
  4.0 0.9 reshape.24.gate
  5.0 0.0 copy-done
  5.0 0.2 copy.15
  5.2 1.0 reshape.25.up
  6.2 333.0 %shard_map.91 = bf16[2,64,7168]{2,1,0:T(8,128)(2,1)} custom-call(f32[16,128]{1,0:T(8,128)} %fusion.meta, bf16[2,64,7168]{2,1,0:T(8,128)(2,1)} %bitcast.23, bf16[16,144,128]{2,1,0:T(8,128)(2,1)} %reshape.24.gate, bf16[16,144,128]{2,1,0:T(8,128)(2,1)} %reshape.25.up, bf16[896,1024]{1,0:T(8,128)(2,1)} %bitcast.24, bf16[896,1024]{1,0:T(8,128)(2,1)} %bitcast.25, ...), custom_call_target="tpu_custom_call" | custom-call | tf_op jit(solution)/shard_map/pallas_call | solution.py:384
  339.2 2.8 copy.17
Async XLA Ops:
  0.0 5.0 %copy-start = (bf16[1,2,1,32,36,128]{5,3,4,2,1,0:T(8,128)(2,1)S(1)}, bf16[1,2,1,32,36,128]{5,3,4,2,1,0:T(8,128)(2,1)}, u32[]{:S(2)}) copy-start(bf16[1,2,1,32,36,128]{5,3,4,2,1,0:T(8,128)(2,1)} %param.14) | copy-start | bytes 1769476
